TPU v7x, 256 devices: a whole 4x4x8 slice. The times are simulated.
256 devices in a mesh: dp: 8 (over z), vocab: 32 (over x, y, core).
Axes of the slice: x: 4, y: 4, z: 8, core: 2. Of those that a mesh axis runs over, the one named last changes fastest.
Arguments:
- hidden: bfloat16 [8, 2, 64, 4608], P('dp'), may hold values from -6 to 6
- table: bfloat16 [73728, 4608], P('vocab', 'dp'), may hold values from -0.25 to 0.25
- new_mask: int32 [73728], P('vocab'), may hold values from 0 to 1, as said below
- labels: int32 [8, 2, 64], P('dp'), may hold values from 0 to 73727
- in_grad: bfloat16 [8, 2, 768, 4608], P('dp', None, 'vocab'), may hold values from -0.75 to 0.75
- item_owner: int32 [8, 2, 768, 1], P('dp', None, 'vocab'), may hold values from 0 to 31; in each aligned block of 24 rows (0 to 23, 24 to 47, ..., all dimensions but the last counted through in order) at most 2 rows name the same one
- item_slot: int32 [8, 2, 768], P('dp', None, 'vocab'), may hold values from 0 to 255
- first_moment: float32 [8192, 4608], P('vocab', 'dp'), may hold values from -0.75 to 0.75
- second_moment: float32 [8192, 4608], P('vocab', 'dp'), may hold values from 0.0001 to 0.01
Outputs:
- token_loss: float32 [8, 2, 64], P('dp')
- d_hidden: bfloat16 [8, 2, 64, 4608], P('dp', None, None, 'vocab')
- update: float32 [8192, 4608], P('vocab', 'dp')
- first_out: float32 [8192, 4608], P('vocab', 'dp')
- second_out: float32 [8192, 4608], P('vocab', 'dp')
Inputs may be any that keep to these rules, and one draw needn't show every extreme that they name: `new_mask`: each aligned block of 2304 entries holds exactly 256 ones. `item_owner`: within the 24 rows of one device in one block, no shard is named more than 2 times, a bound that some block reaches.
All inputs are finite; a program needn't handle non-finite values.
Results may differ from a plain program's by a relative error of at most 0.006.
Values may be sent and summed in bfloat16 or wider, within the bound.
No kernel may reach another device: no remote copies, remote signals or barrier semaphores. Data moves between devices by JAX's collectives and lax.ppermute only.
A program may use at most 128 MiB of HBM per device.

v0:
```python
import jax
import jax.numpy as jnp
from jax import lax
from jax.sharding import PartitionSpec as P

cap_value = 30.0
beta_one = 0.9
beta_two = 0.95
step_count = 10
epsilon = 1e-08
decay_rate = 0.1


def sent_to_all(array, axis):
    peers = lax.axis_size(axis)
    return lax.all_to_all(
        jnp.broadcast_to(array[None], (peers, *array.shape)), axis, 0, 0, tiled=True
    )


def over_copies(array, axis):
    return sent_to_all(array, axis).sum(axis=0)


def packed_total(arrays, axis):
    line, at, gathered = (jnp.concatenate([a.reshape(-1) for a in arrays]), 0, [])
    subtotal = over_copies(line, axis)
    for a in arrays:
        gathered.append(subtotal[at : at + a.size].reshape(a.shape))
        at += a.size
    return tuple(gathered)


def in_blocks(array, dim, peers):
    shape = array.shape
    parts = array.reshape(*shape[:dim], peers, shape[dim] // peers, *shape[dim + 1 :])
    return jnp.moveaxis(parts, dim, 0)


def sent_and_summed(array, axis, dim):
    parts = in_blocks(array, dim, lax.axis_size(axis))
    arrived = lax.all_to_all(parts, axis, split_axis=0, concat_axis=0, tiled=True)
    return arrived.sum(axis=0)


def select_rows(new_mask, new_count):
    ranked = jnp.cumsum(new_mask) - 1
    wanted = (ranked[None, :] == jnp.arange(new_count, dtype=jnp.int32)[:, None]) & (
        new_mask[None, :] == 1
    )
    return wanted.astype(jnp.bfloat16)


def softmax_error(raw, label_row, vocab_start):
    capped = cap_value * jnp.tanh(raw / cap_value)
    expd = jnp.exp(capped)
    hits = jnp.arange(raw.shape[1], dtype=jnp.int32)[None, :] + vocab_start == label_row[:, None]
    local_total = jnp.sum(expd, axis=1)
    local_pick = jnp.sum(jnp.where(hits, capped, 0.0), axis=1)
    total, picked = packed_total((local_total, local_pick), "vocab")
    loss = jnp.log(total) - picked
    error = (
        (expd / total[:, None] - hits.astype(jnp.float32)) * (1.0 - (capped / cap_value) ** 2)
    ).astype(jnp.bfloat16)
    return (loss, error)


def finish_hidden(partial_value):
    return sent_and_summed(partial_value, "vocab", 1).astype(jnp.bfloat16)


def pack_items(rows, owner, slot, shards, capacity):
    onehot = (owner[:, None] == jnp.arange(shards, dtype=jnp.int32)[None, :]).astype(jnp.int32)
    running = jnp.cumsum(onehot, axis=0)
    ranked = jnp.sum(onehot * running, axis=1) - 1
    place = owner * capacity + ranked
    placing = jnp.arange(shards * capacity, dtype=jnp.int32)[:, None] == place[None, :]
    sent = jnp.dot(placing.astype(jnp.bfloat16), rows, preferred_element_type=jnp.float32).astype(
        jnp.bfloat16
    )
    targets = jnp.sum(placing.astype(jnp.int32) * (slot + 1)[None, :], axis=1) - 1
    return (sent.reshape(shards, capacity, rows.shape[1]), targets.reshape(shards, capacity))


def scatter_items(rows, targets, new_count):
    picking = (jnp.arange(new_count, dtype=jnp.int32)[:, None] == targets[None, :]).astype(
        jnp.bfloat16
    )
    return jnp.dot(picking, rows, preferred_element_type=jnp.float32)


def body(
    hidden, table, new_mask, labels, in_grad, item_owner, item_slot, first_moment, second_moment
):
    blocks = hidden.shape[1]
    width = hidden.shape[3]
    new_count = first_moment.shape[0]
    shards = lax.axis_size("vocab")
    items_here = in_grad.shape[2]
    capacity = max(2, (2 * items_here + shards - 1) // shards)
    vocab_start = lax.axis_index("vocab") * table.shape[0]
    select = select_rows(new_mask, new_count)
    params = jnp.dot(select, table, preferred_element_type=jnp.float32)
    received_rows = []
    received_targets = []
    losses = []
    dstates = []
    full_table = lax.all_gather(table, "dp", axis=1, tiled=True)
    grads = jnp.zeros((new_count, width), jnp.float32)
    for c in range(blocks):
        states = hidden[0, c]
        raw = lax.dot_general(
            states, full_table, (((1,), (1,)), ((), ())), preferred_element_type=jnp.float32
        )
        loss, error = softmax_error(raw, labels[0, c], vocab_start)
        partial_value = jnp.dot(error, full_table, preferred_element_type=jnp.float32)
        dstates.append(finish_hidden(partial_value))
        chosen = lax.dot_general(
            error, select, (((1,), (1,)), ((), ())), preferred_element_type=jnp.float32
        ).astype(jnp.bfloat16)
        grads = grads + lax.dot_general(
            chosen, states, (((0,), (0,)), ((), ())), preferred_element_type=jnp.float32
        )
        losses.append(loss)
        sent_rows, sent_targets = pack_items(
            in_grad[0, c], item_owner[0, c, :, 0], item_slot[0, c], shards, capacity
        )
        got_rows, got_targets = (
            lax.all_to_all(sent_rows, "vocab", split_axis=0, concat_axis=0, tiled=True),
            lax.all_to_all(sent_targets, "vocab", split_axis=0, concat_axis=0, tiled=True),
        )
        received_rows.append(got_rows.reshape(-1, width))
        received_targets.append(got_targets.reshape(-1))
    item_rows = jnp.concatenate(received_rows, axis=0)
    item_targets = jnp.concatenate(received_targets, axis=0)
    grads = grads + scatter_items(item_rows, item_targets, new_count)
    grads = lax.psum_scatter(grads, "dp", scatter_dimension=1, tiled=True)
    first_out = beta_one * first_moment + (1.0 - beta_one) * grads
    second_out = beta_two * second_moment + (1.0 - beta_two) * grads * grads
    update = (
        first_out
        / (1.0 - beta_one**step_count)
        / (jnp.sqrt(second_out / (1.0 - beta_two**step_count)) + epsilon)
        + decay_rate * params
    )
    token_loss = jnp.stack(losses)[None]
    d_hidden = jnp.stack(dstates)[None]
    return (token_loss, d_hidden, update, first_out, second_out)


def solution(mesh):
    return jax.shard_map(
        body,
        mesh=mesh,
        in_specs=(
            P("dp", None, None, None),
            P("vocab", "dp"),
            P("vocab"),
            P("dp", None, None),
            P("dp", None, "vocab", None),
            P("dp", None, "vocab", None),
            P("dp", None, "vocab"),
            P("vocab", "dp"),
            P("vocab", "dp"),
        ),
        out_specs=(
            P("dp", None, None),
            P("dp", None, None, "vocab"),
            P("vocab", "dp"),
            P("vocab", "dp"),
            P("vocab", "dp"),
        ),
        check_vma=False,
    )
```

profile of v0, /device:TPU:1, one launch (start us, length us, event | category | flops | bytes accessed | tf_op | source)
XLA Modules:
  0.0 393.1 jit_solution(2182474801881133417)
XLA Ops:
  7.3 0.7 all-gather.2.cloned.1.call-update
  8.5 0.7 sub.53
  9.2 8.6 %all-to-all-start.5 = ((s32[32,1,2]{2,1,0:T(1,128)}), s32[32,1,2]{2,1,0:T(1,128)S(1)}, u32[]{:S(2)}, u32[]{:S(2)}) async-start(s32[32,1,2]{2,1,0:T(1,128)} %bitcast.21), calls=%async_computation.5 | async-start | bytes 32768 | tf_op jit(solution)/shard_map/all_to_all | solution.py:130
  17.8 0.3 reduce-window.9
  18.6 0.4 convolution_convert_fusion
  19.0 0.4 convolution_convert_fusion.1
  19.5 0.7 sub.50
  20.2 4.6 %all-to-all-done.5 = s32[32,1,2]{2,1,0:T(1,128)S(1)} async-done(((s32[32,1,2]{2,1,0:T(1,128)}), s32[32,1,2]{2,1,0:T(1,128)S(1)}, u32[]{:S(2)}, u32[]{:S(2)}) %all-to-all-start.5) | async-done | bytes 288 | tf_op jit(solution)/shard_map/all_to_all | solution.py:130
  24.7 4.1 %all-to-all-start.4 = ((s32[32,1,2]{2,1,0:T(1,128)}), s32[32,1,2]{2,1,0:T(1,128)S(1)}, u32[]{:S(2)}, u32[]{:S(2)}) async-start(s32[32,1,2]{2,1,0:T(1,128)} %bitcast.18), calls=%async_computation.4 | async-start | bytes 32768 | tf_op jit(solution)/shard_map/all_to_all | solution.py:130
  28.9 1.0 reshape.176
  29.9 1.0 reshape.174
  30.9 0.5 broadcast.174
  31.5 0.7 reduce.10
  32.3 3.6 all-to-all-done.4
  35.9 4.2 %all-to-all-start.7 = ((bf16[32,2,4608]{2,1,0:T(2,128)(2,1)}), bf16[32,2,4608]{2,1,0:T(2,128)(2,1)S(1)}, u32[]{:S(2)}, u32[]{:S(2)}) async-start(bf16[32,2,4608]{2,1,0:T(2,128)(2,1)} %reshape.176), calls=%async_computation.7 | async-start | bytes 1179648 | tf_op jit(solution)/shard_map/all_to_all | solution.py:129
  40.1 0.7 reduce.11
  40.9 187.1 %all-gather.2.cloned.1.call-done = bf16[2304,4608]{0,1:T(8,128)(2,1)} async-done(((bf16[2304,576]{0,1:T(8,128)(2,1)}), bf16[2304,4608]{0,1:T(8,128)(2,1)}) %all-gather.2.cloned.1.call-update) | async-done | bytes 21233680 | tf_op jit(solution)/shard_map/all_gather | solution.py:108
  228.0 9.1 %fusion.1 = f32[64,2304]{1,0:T(8,128)S(1)} fusion(bf16[2304,4608]{0,1:T(8,128)(2,1)} %all-gather.2.cloned.1.call-done, bf16[1,2,64,4608]{3,2,1,0:T(8,128)(2,1)S(1)} %copy-done), kind=kOutput, calls=%fused_computation.7 | convolution fusion | flops 1359101952 | bytes 22413312 | tf_op jit(solution)/shard_map/dot_general | solution.py:112
  237.1 7.8 %all-to-all-start.6 = ((bf16[32,2,4608]{2,1,0:T(2,128)(2,1)}), bf16[32,2,4608]{2,1,0:T(2,128)(2,1)}, u32[]{:S(2)}, u32[]{:S(2)}) async-start(bf16[32,2,4608]{2,1,0:T(2,128)(2,1)} %reshape.174), calls=%async_computation.6 | async-start | bytes 1179648 | tf_op jit(solution)/shard_map/all_to_all | solution.py:129
  244.9 9.2 %exponential_reduce_fusion.1 = (f32[64]{0:T(128)S(1)}, f32[64]{0:T(128)S(1)}, f32[64]{0:T(128)S(1)}, f32[64]{0:T(128)S(1)}, f32[64,2304]{1,0:T(8,128)S(1)}) fusion(s32[64]{0:T(128)S(1)} %get-tuple-element.19, s32[2304]{0:T(1024)S(1)} %iota_add_fusion, s32[64]{0:T(128)S(1)} %get-tuple-element.20, f32[64,2304]{1,0:T(8,128)S(1)} %fusion.1, ...), kind=kOutput, calls=%fused_computation.49 | convolution fusion | flops 1360576512 | bytes 23017472 | tf_op jit(solution)/shard_map/dot_general | solution.py:112
  254.2 3.0 all-to-all-done.6
  257.2 0.6 broadcast_in_dim.15
  257.8 4.4 %all-to-all-start.1 = ((f32[32,1,128]{2,1,0:T(1,128)}), f32[32,1,128]{2,1,0:T(1,128)S(1)}, u32[]{:S(2)}, u32[]{:S(2)}) async-start(f32[32,1,128]{2,1,0:T(1,128)} %broadcast_in_dim.15), calls=%async_computation.1 | async-start | bytes 32768 | tf_op jit(solution)/shard_map/all_to_all | solution.py:16
  262.3 6.8 %all-to-all-done.1 = f32[32,1,128]{2,1,0:T(1,128)S(1)} async-done(((f32[32,1,128]{2,1,0:T(1,128)}), f32[32,1,128]{2,1,0:T(1,128)S(1)}, u32[]{:S(2)}, u32[]{:S(2)}) %all-to-all-start.1) | async-done | bytes 16416 | tf_op jit(solution)/shard_map/all_to_all | solution.py:16
  269.1 0.6 broadcast_in_dim.14
  269.7 4.1 %all-to-all-start = ((f32[32,1,128]{2,1,0:T(1,128)}), f32[32,1,128]{2,1,0:T(1,128)S(1)}, u32[]{:S(2)}, u32[]{:S(2)}) async-start(f32[32,1,128]{2,1,0:T(1,128)} %broadcast_in_dim.14), calls=%async_computation | async-start | bytes 32768 | tf_op jit(solution)/shard_map/all_to_all | solution.py:16
  273.8 0.2 reduce-scatter.2.cloned.1.call-start
  274.2 1.0 reshape.177
  275.2 2.1 reshape.175
  277.3 3.5 all-to-all-done
  281.0 4.1 %fusion.33 = f32[256,4608]{0,1:T(8,128)} fusion(s32[2304]{0:T(1024)S(1)} %add_bitcast_fusion, pred[2304]{0:T(1024)(128)(4,1)S(1)} %broadcast_compare_fusion, bf16[1,2,64,4608]{3,2,1,0:T(8,128)(2,1)S(1)} %copy-done, f32[64,2304]{1,0:T(8,128)S(1)} %get-tuple-element.25, f32[64]{0:T(128)S(1)} %get-tuple-element.21, s32[2304]{0:T(1024)S(1)} %iota_add_fusion, ...), kind=kOutput, calls=%fused_computation.28 | convolution fusion | flops 229015552 | bytes 5926912 | tf_op jit(solution)/shard_map/dot_general | solution.py:121
  285.0 6.5 %convolution_add_fusion.1 = f32[256,4608]{0,1:T(8,128)} fusion(f32[256,4608]{0,1:T(8,128)} %fusion.33, s32[2304]{0:T(1024)S(1)} %add_bitcast_fusion, pred[2304]{0:T(1024)(128)(4,1)S(1)} %broadcast_compare_fusion, bf16[1,2,64,4608]{3,2,1,0:T(8,128)(2,1)S(1)} %copy-done, f32[64,2304]{1,0:T(8,128)S(1)} %fusion.1, f32[64]{0:T(128)S(1)} %get-tuple-element.27, ...), kind=kOutput, calls=%fused_computation.1 | convolution fusion | flops 230195200 | bytes 10645504 | tf_op jit(solution)/shard_map/dot_general | solution.py:121
  291.5 5.5 %convolution_add_fusion = f32[256,4608]{0,1:T(8,128)} fusion(f32[256,4608]{0,1:T(8,128)} %convolution_add_fusion.1, bf16[64,4608]{1,0:T(8,128)(2,1)S(1)} %copy-done.2, bf16[64,4608]{1,0:T(8,128)(2,1)} %reshape.175, s32[128]{0:T(128)S(1)} %pad_add_fusion), kind=kOutput, calls=%fused_computation | convolution fusion | flops 305561600 | bytes 10617344 | tf_op jit(solution)/shard_map/dot_general | solution.py:89
  297.1 11.7 %fusion.64 = f32[64,4608]{1,0:T(8,128)} fusion(bf16[2304,4608]{0,1:T(8,128)(2,1)} %all-gather.2.cloned.1.call-done, f32[64,2304]{1,0:T(8,128)S(1)} %fusion.1, f32[64]{0:T(128)S(1)} %get-tuple-element.27, s32[2304]{0:T(1024)S(1)} %iota_add_fusion, s32[64]{0:T(128)S(1)} %get-tuple-element.20), kind=kOutput, calls=%fused_computation.96 | convolution fusion | flops 1360281600 | bytes 23012864 | tf_op jit(solution)/shard_map/dot_general | solution.py:116
  308.8 2.7 reshape.169
  311.6 2.5 copy.30
  314.1 4.3 %all-to-all-start.3 = ((f32[32,64,144]{2,1,0:T(8,128)}), f32[32,64,144]{2,1,0:T(8,128)S(1)}, u32[]{:S(2)}, u32[]{:S(2)}) async-start(f32[32,64,144]{2,1,0:T(8,128)} %bitcast.67), calls=%async_computation.3 | async-start | bytes 4194304 | tf_op jit(solution)/shard_map/all_to_all | solution.py:42
  318.4 11.9 %fusion.68 = f32[64,4608]{1,0:T(8,128)} fusion(bf16[2304,4608]{0,1:T(8,128)(2,1)} %all-gather.2.cloned.1.call-done, f32[64,2304]{1,0:T(8,128)S(1)} %get-tuple-element.25, f32[64]{0:T(128)S(1)} %get-tuple-element.21, s32[2304]{0:T(1024)S(1)} %iota_add_fusion, s32[64]{0:T(128)S(1)} %get-tuple-element.19), kind=kOutput, calls=%fused_computation.97 | convolution fusion | flops 1360281600 | bytes 23012864 | tf_op jit(solution)/shard_map/dot_general | solution.py:116
  330.3 3.6 reshape.168
  333.9 4.2 %copy.31 = f32[64,32,144]{2,0,1:T(8,128)} copy(f32[64,32,144]{2,1,0:T(8,128)} %reshape.168) | data formatting | bytes 2359296 | tf_op jit(solution)/shard_map/reshape | solution.py:36
  338.1 8.7 %all-to-all-done.3 = f32[32,64,144]{2,1,0:T(8,128)S(1)} async-done(((f32[32,64,144]{2,1,0:T(8,128)}), f32[32,64,144]{2,1,0:T(8,128)S(1)}, u32[]{:S(2)}, u32[]{:S(2)}) %all-to-all-start.3) | async-done | bytes 1179680 | tf_op jit(solution)/shard_map/all_to_all | solution.py:42
  346.9 5.2 %all-to-all-start.2 = ((f32[32,64,144]{2,1,0:T(8,128)}), f32[32,64,144]{2,1,0:T(8,128)}, u32[]{:S(2)}, u32[]{:S(2)}) async-start(f32[32,64,144]{2,1,0:T(8,128)} %bitcast.66), calls=%async_computation.2 | async-start | bytes 4194304 | tf_op jit(solution)/shard_map/all_to_all | solution.py:42
  352.1 0.6 maximum_bitcast_fusion.1
  352.8 27.7 %all-to-all-done.2 = f32[32,64,144]{2,1,0:T(8,128)} async-done(((f32[32,64,144]{2,1,0:T(8,128)}), f32[32,64,144]{2,1,0:T(8,128)}, u32[]{:S(2)}, u32[]{:S(2)}) %all-to-all-start.2) | async-done | bytes 1179680 | tf_op jit(solution)/shard_map/all_to_all | solution.py:42
  380.5 1.7 reduce_sum.114
  382.3 0.6 maximum_bitcast_fusion
  382.9 1.4 multiply_add_fusion
  384.4 1.9 fusion.12
  (54 shorter events, 1.7 us)
Async XLA Ops:
  7.2 0.8 copy-start.8
  7.2 1.2 copy-start.9
  7.2 10.6 %copy-start.7 = (s32[2304]{0:T(1024)S(1)}, s32[2304]{0:T(1024)}, u32[]{:S(2)}) copy-start(s32[2304]{0:T(1024)} %param.11) | copy-start | bytes 27652
  7.2 11.3 %copy-start.10 = (s32[1,2,64]{2,1,0:T(2,128)S(1)}, s32[1,2,64]{2,1,0:T(2,128)}, u32[]{:S(2)}) copy-start(s32[1,2,64]{2,1,0:T(2,128)} %param.12) | copy-start | bytes 1540
  7.2 11.4 %copy-start.6 = (bf16[1,2,24,4608]{3,2,1,0:T(8,128)(2,1)S(1)}, bf16[1,2,24,4608]{3,2,1,0:T(8,128)(2,1)}, u32[]{:S(2)}) copy-start(bf16[1,2,24,4608]{3,2,1,0:T(8,128)(2,1)} %param.13) | copy-start | bytes 1327108
  7.2 220.8 %all-gather.2.cloned.1.call-start = ((), (), s32[]{:S(2)}) async-start(), calls=%async_computation.9 | async-start | bytes 23887872 | tf_op jit(solution)/shard_map/all_gather | solution.py:108
  9.2 15.5 %all-to-all-start.5 = ((s32[32,1,2]{2,1,0:T(1,128)}), s32[32,1,2]{2,1,0:T(1,128)S(1)}, u32[]{:S(2)}, u32[]{:S(2)}) async-start(s32[32,1,2]{2,1,0:T(1,128)} %bitcast.21), calls=%async_computation.5 | async-start | bytes 32768 | tf_op jit(solution)/shard_map/all_to_all | solution.py:130
  19.0 209.0 %copy-start = (bf16[1,2,64,4608]{3,2,1,0:T(8,128)(2,1)S(1)}, bf16[1,2,64,4608]{3,2,1,0:T(8,128)(2,1)}, u32[]{:S(2)}) copy-start(bf16[1,2,64,4608]{3,2,1,0:T(8,128)(2,1)} %param.9) | copy-start | bytes 3538948
  24.7 11.2 %all-to-all-start.4 = ((s32[32,1,2]{2,1,0:T(1,128)}), s32[32,1,2]{2,1,0:T(1,128)S(1)}, u32[]{:S(2)}, u32[]{:S(2)}) async-start(s32[32,1,2]{2,1,0:T(1,128)} %bitcast.18), calls=%async_computation.4 | async-start | bytes 32768 | tf_op jit(solution)/shard_map/all_to_all | solution.py:130
  35.9 201.2 %all-to-all-start.7 = ((bf16[32,2,4608]{2,1,0:T(2,128)(2,1)}), bf16[32,2,4608]{2,1,0:T(2,128)(2,1)S(1)}, u32[]{:S(2)}, u32[]{:S(2)}) async-start(bf16[32,2,4608]{2,1,0:T(2,128)(2,1)} %reshape.176), calls=%async_computation.7 | async-start | bytes 1179648 | tf_op jit(solution)/shard_map/all_to_all | solution.py:129
  237.1 20.1 %all-to-all-start.6 = ((bf16[32,2,4608]{2,1,0:T(2,128)(2,1)}), bf16[32,2,4608]{2,1,0:T(2,128)(2,1)}, u32[]{:S(2)}, u32[]{:S(2)}) async-start(bf16[32,2,4608]{2,1,0:T(2,128)(2,1)} %reshape.174), calls=%async_computation.6 | async-start | bytes 1179648 | tf_op jit(solution)/shard_map/all_to_all | solution.py:129
  257.8 11.3 %all-to-all-start.1 = ((f32[32,1,128]{2,1,0:T(1,128)}), f32[32,1,128]{2,1,0:T(1,128)S(1)}, u32[]{:S(2)}, u32[]{:S(2)}) async-start(f32[32,1,128]{2,1,0:T(1,128)} %broadcast_in_dim.15), calls=%async_computation.1 | async-start | bytes 32768 | tf_op jit(solution)/shard_map/all_to_all | solution.py:16
  269.7 11.2 %all-to-all-start = ((f32[32,1,128]{2,1,0:T(1,128)}), f32[32,1,128]{2,1,0:T(1,128)S(1)}, u32[]{:S(2)}, u32[]{:S(2)}) async-start(f32[32,1,128]{2,1,0:T(1,128)} %broadcast_in_dim.14), calls=%async_computation | async-start | bytes 32768 | tf_op jit(solution)/shard_map/all_to_all | solution.py:16
  273.8 109.1 %reduce-scatter.2.cloned.1.call-start = ((), (), s32[]{:S(2)}) async-start(), calls=%async_computation.10 | async-start | bytes 5308416 | tf_op jit(solution)/shard_map/reduce_scatter | solution.py:137
  285.0 6.5 %copy-start.2 = (bf16[64,4608]{1,0:T(8,128)(2,1)S(1)}, bf16[64,4608]{1,0:T(8,128)(2,1)}, u32[]{:S(2)}) copy-start(bf16[64,4608]{1,0:T(8,128)(2,1)} %reshape.177) | copy-start | bytes 1769476
  314.1 32.8 %all-to-all-start.3 = ((f32[32,64,144]{2,1,0:T(8,128)}), f32[32,64,144]{2,1,0:T(8,128)S(1)}, u32[]{:S(2)}, u32[]{:S(2)}) async-start(f32[32,64,144]{2,1,0:T(8,128)} %bitcast.67), calls=%async_computation.3 | async-start | bytes 4194304 | tf_op jit(solution)/shard_map/all_to_all | solution.py:42
  346.9 33.6 %all-to-all-start.2 = ((f32[32,64,144]{2,1,0:T(8,128)}), f32[32,64,144]{2,1,0:T(8,128)}, u32[]{:S(2)}, u32[]{:S(2)}) async-start(f32[32,64,144]{2,1,0:T(8,128)} %bitcast.66), calls=%async_computation.2 | async-start | bytes 4194304 | tf_op jit(solution)/shard_map/all_to_all | solution.py:42
  352.0 30.9 %copy-start.3 = (f32[256,576]{0,1:T(8,128)S(1)}, f32[256,576]{0,1:T(8,128)}, u32[]{:S(2)}) copy-start(f32[256,576]{0,1:T(8,128)} %param.16) | copy-start | bytes 1769476
  352.8 31.6 %copy-start.1 = (bf16[2304,576]{0,1:T(8,128)(2,1)S(1)}, bf16[2304,576]{0,1:T(8,128)(2,1)}, u32[]{:S(2)}) copy-start(bf16[2304,576]{0,1:T(8,128)(2,1)} %param.10) | copy-start | bytes 7962628
  384.3 1.9 copy-start.4
  384.3 1.9 copy-start.5
Sparse Core Ops, SparseCore 0:
  9.8 218.1 all-gather.1
  297.2 55.2 reduce-scatter.1
where the time goes:
time: 394 us; the launch traced here: 393 us
  waiting for transfers between devices  246 us (62%)
  matrix products  60.8 us (15%)
  starting transfers between devices  43 us (11%)
  local copies, waits for them, and re-layouts  21.9 us (6%)
  between operations  14.4 us (4%)
  other arithmetic  7.26 us (2%)
    all_gather x1, waiting for transfers between devices, body(): full_table = lax.all_gather(table, 'dp', axis=1, tiled=True)  187 us
    all_to_all x2, waiting for transfers between devices, sent_and_summed(): lax.all_to_all(parts, axis, split_axis=0, concat_axis=0, tiled=True)  36.5 us
    dot_general x2, matrix products, body(): jnp.dot(error, full_table, preferred_element_type=jnp.float32)  23.6 us
    dot_general x2, matrix products, body(): lax.dot_general(states, full_table, (((1,), (1,)), ((), ())), preferred_e...  18.3 us
    reshape x4, local copies, waits for them, and re-layouts, in_blocks(): array.reshape(*shape[:dim], peers, shape[dim] // peers, *shape[dim + 1:])  13.1 us
    all_to_all x2, starting transfers between devices, body(): lax.all_to_all(sent_targets, 'vocab', split_axis=0, concat_axis=0, tiled=...  12.7 us
    all_to_all x2, starting transfers between devices, body(): lax.all_to_all(sent_rows, 'vocab', split_axis=0, concat_axis=0, tiled=True)  12 us
    dot_general x2, matrix products, body(): lax.dot_general(chosen, states, (((0,), (0,)), ((), ())), preferred_eleme...  10.6 us
  transfers between devices with their start and end apart: 10, of which 8 were waited for; matrix products, arithmetic and copies ran while one was open for 18% of the time, Pallas kernels for 0%

commit v1 on v0

--- a/solution.py
+++ b/solution.py
@@ -105,7 +105,15 @@
     received_targets = []
     losses = []
     dstates = []
-    full_table = lax.all_gather(table, "dp", axis=1, tiled=True)
+
+    def edges_arrange(block_in, row_axis):
+        carry_out = jnp.concatenate([block_in for _ in range(lax.psum(1, row_axis))], axis=1)
+        x_now = lax.all_to_all(
+            carry_out, tiled=True, concat_axis=1, axis_name=row_axis, split_axis=1
+        )
+        return x_now
+
+    full_table = edges_arrange(table, "dp")
     grads = jnp.zeros((new_count, width), jnp.float32)
     for c in range(blocks):
         states = hidden[0, c]

time: 394 us -> 691 us (1.75)
  waiting for transfers between devices: 246 us -> 515 us
  starting transfers between devices: 43 us -> 55.2 us
  matrix products: 60.8 us -> 70 us
    all_to_all x0 -> x1, waiting for transfers between devices: none -> 456 us  [edges_arrange(): lax.all_to_all(carry_out, tiled=True, concat_axis=1, axis_name=row_axis,...]
    all_gather x1 -> x0, waiting for transfers between devices: 187 us -> none  [body(): full_table = lax.all_gather(table, 'dp', axis=1, tiled=True)]
    unnamed x22 -> x19, local copies, waits for them, and re-layouts: 0.05 us -> 13.5 us
    reshape x4 -> x0, local copies, waits for them, and re-layouts: 13.1 us -> none  [in_blocks(): array.reshape(*shape[:dim], peers, shape[dim] // peers, *shape[dim + 1:])]
    all_to_all x0 -> x1, starting transfers between devices: none -> 8.32 us  [edges_arrange(): lax.all_to_all(carry_out, tiled=True, concat_axis=1, axis_name=row_axis,...]
  transfers between devices with their start and end apart: 10 -> 10, of which waited for: 8 -> 7; matrix products, arithmetic and copies ran while one was open for 18% -> 12% of each run, Pallas kernels for 0% -> 0%
where the time goes in v1:
time: 691 us; the launch traced here: 690 us
  waiting for transfers between devices  515 us (75%)
  matrix products  70 us (10%)
  starting transfers between devices  55.2 us (8%)
  local copies, waits for them, and re-layouts  25.9 us (4%)
  between operations  14.2 us (2%)
  other arithmetic  10.3 us (1%)
    all_to_all x1, waiting for transfers between devices, edges_arrange(): lax.all_to_all(carry_out, tiled=True, concat_axis=1, axis_name=row_axis,...  456 us
    all_to_all x2, waiting for transfers between devices, sent_and_summed(): lax.all_to_all(parts, axis, split_axis=0, concat_axis=0, tiled=True)  40.8 us
    dot_general x2, matrix products, body(): jnp.dot(error, full_table, preferred_element_type=jnp.float32)  26.5 us
    dot_general x2, matrix products, body(): lax.dot_general(states, full_table, (((1,), (1,)), ((), ())), preferred_e...  21.3 us
    all_to_all x2, starting transfers between devices, body(): lax.all_to_all(sent_targets, 'vocab', split_axis=0, concat_axis=0, tiled=...  16 us
  transfers between devices with their start and end apart: 10, of which 7 were waited for; matrix products, arithmetic and copies ran while one was open for 12% of the time, Pallas kernels for 0%

profile of v1, /device:TPU:1, one launch (start us, length us, event | category | flops | bytes accessed | tf_op | source)
XLA Modules:
  0.0 690.2 jit_solution(4353950227982446252)
XLA Ops:
  7.2 0.8 slice_bitcast_fusion.1
  8.2 0.8 add_bitcast_fusion.2
  9.2 0.7 add_add_fusion.1
  10.0 0.7 sub.58
  10.7 8.6 %all-to-all-start.5 = ((s32[32,1,2]{2,1,0:T(1,128)}), s32[32,1,2]{2,1,0:T(1,128)S(1)}, u32[]{:S(2)}, u32[]{:S(2)}) async-start(s32[32,1,2]{2,1,0:T(1,128)} %bitcast.30), calls=%async_computation.5 | async-start | bytes 32768 | tf_op jit(solution)/shard_map/all_to_all | solution.py:138
  19.3 3.4 constant_dynamic-update-slice_fusion.7
  22.7 1.7 constant_dynamic-update-slice_fusion.6
  24.4 1.6 constant_dynamic-update-slice_fusion.5
  26.1 1.7 constant_dynamic-update-slice_fusion.4
  27.8 1.6 constant_dynamic-update-slice_fusion.3
  29.4 1.7 constant_dynamic-update-slice_fusion.2
  31.1 1.6 constant_dynamic-update-slice_fusion.1
  32.8 0.7 sub.61
  33.6 7.4 %all-to-all-start.6 = ((s32[32,1,2]{2,1,0:T(1,128)}), s32[32,1,2]{2,1,0:T(1,128)S(1)}, u32[]{:S(2)}, u32[]{:S(2)}) async-start(s32[32,1,2]{2,1,0:T(1,128)} %bitcast.33), calls=%async_computation.6 | async-start | bytes 32768 | tf_op jit(solution)/shard_map/all_to_all | solution.py:138
  41.0 1.7 constant_dynamic-update-slice_fusion
  42.7 5.2 all-to-all-done.6
  47.9 8.3 %all-to-all-start = ((bf16[2304,8,576]{0,2,1:T(8,128)(2,1)}), bf16[2304,8,576]{0,2,1:T(8,128)(2,1)}, u32[]{:S(2)}, u32[]{:S(2)}) async-start(bf16[2304,8,576]{0,2,1:T(8,128)(2,1)} %bitcast), calls=%async_computation | async-start | bytes 42467328 | tf_op jit(solution)/shard_map/all_to_all | solution.py:111
  56.6 1.4 convolution_convert_fusion.1
  57.9 1.0 reshape.172
  59.0 1.4 convolution_convert_fusion
  60.3 1.0 reshape.174
  62.1 0.7 reduce.11
  62.9 0.7 reduce.10
  63.7 455.9 %all-to-all-done = bf16[2304,8,576]{0,2,1:T(8,128)(2,1)} async-done(((bf16[2304,8,576]{0,2,1:T(8,128)(2,1)}), bf16[2304,8,576]{0,2,1:T(8,128)(2,1)}, u32[]{:S(2)}, u32[]{:S(2)}) %all-to-all-start) | async-done | bytes 21233696 | tf_op jit(solution)/shard_map/all_to_all | solution.py:111
  519.6 4.7 all-to-all-start.7
  524.3 9.2 %fusion.1 = f32[2304,64]{0,1:T(8,128)S(1)} fusion(bf16[2304,4608]{0,1:T(8,128)(2,1)} %bitcast.1, bf16[1,2,64,4608]{3,2,1,0:T(8,128)(2,1)} %param.9), kind=kOutput, calls=%fused_computation.7 | convolution fusion | flops 1359101952 | bytes 22413312 | tf_op jit(solution)/shard_map/dot_general | solution.py:120
  533.5 3.2 all-to-all-done.7
  536.7 4.4 all-to-all-start.8
  541.1 12.1 %fusion.48 = (f32[64]{0:T(128)S(1)}, f32[64]{0:T(128)S(1)}, f32[64]{0:T(128)S(1)}, f32[64]{0:T(128)S(1)}, f32[2304,64]{0,1:T(8,128)}) fusion(s32[64]{0:T(128)S(1)} %get-tuple-element.19, s32[2304]{0:T(1024)S(1)} %iota_add_fusion, s32[64]{0:T(128)S(1)} %get-tuple-element.20, f32[2304,64]{0,1:T(8,128)S(1)} %fusion.1, bf16[2304,4608]{0,1:T(8,128)(2,1)} %bitcast.1, ...), kind=kOutput, calls=%fused_computation.50 | convolution fusion | flops 1360576512 | bytes 23013888 | tf_op jit(solution)/shard_map/dot_general | solution.py:120
  554.0 7.3 %all-to-all-start.2 = ((f32[32,1,128]{2,1,0:T(1,128)}), f32[32,1,128]{2,1,0:T(1,128)S(1)}, u32[]{:S(2)}, u32[]{:S(2)}) async-start(f32[32,1,128]{2,1,0:T(1,128)} %broadcast_in_dim.15), calls=%async_computation.2 | async-start | bytes 32768 | tf_op jit(solution)/shard_map/all_to_all | solution.py:16
  561.4 6.8 all-to-all-done.2
  568.8 4.1 all-to-all-start.1
  573.2 2.1 reshape.173
  575.3 2.1 reshape.175
  577.5 2.5 all-to-all-done.1
  580.0 5.3 fusion.33
  585.4 6.6 convolution_add_fusion.1
  592.0 5.7 convolution_add_fusion
  597.7 12.8 %convolution_bitcast_fusion.1 = f32[32,64,144]{2,1,0:T(8,128)} fusion(bf16[32,144,2304]{2,1,0:T(8,128)(2,1)} %bitcast.16, f32[2304,64]{0,1:T(8,128)} %get-tuple-element.25, f32[64]{0:T(128)S(1)} %get-tuple-element.21, s32[2304]{0:T(1024)S(1)} %iota_add_fusion, s32[64]{0:T(128)S(1)} %get-tuple-element.19), kind=kOutput, calls=%fused_computation.14 | convolution fusion | flops 1360281600 | bytes 23012864 | tf_op jit(solution)/shard_map/dot_general | solution.py:124
  610.5 5.1 all-to-all-start.3
  615.6 13.7 %convolution_bitcast_fusion = f32[32,64,144]{2,1,0:T(8,128)} fusion(bf16[32,144,2304]{2,1,0:T(8,128)(2,1)} %bitcast.16, f32[2304,64]{0,1:T(8,128)S(1)} %fusion.1, f32[64]{0:T(128)S(1)} %get-tuple-element.27, s32[2304]{0:T(1024)S(1)} %iota_add_fusion, s32[64]{0:T(128)S(1)} %get-tuple-element.20), kind=kOutput, calls=%fused_computation.13 | convolution fusion | flops 1360281600 | bytes 23012864 | tf_op jit(solution)/shard_map/dot_general | solution.py:124
  629.3 14.7 %all-to-all-done.3 = f32[32,64,144]{2,1,0:T(8,128)} async-done(((f32[32,64,144]{2,1,0:T(8,128)}), f32[32,64,144]{2,1,0:T(8,128)}, u32[]{:S(2)}, u32[]{:S(2)}) %all-to-all-start.3) | async-done | bytes 1179680 | tf_op jit(solution)/shard_map/all_to_all | solution.py:42
  644.0 5.2 all-to-all-start.4
  649.7 1.8 reduce_sum.114
  651.5 26.1 %all-to-all-done.4 = f32[32,64,144]{2,1,0:T(8,128)} async-done(((f32[32,64,144]{2,1,0:T(8,128)}), f32[32,64,144]{2,1,0:T(8,128)}, u32[]{:S(2)}, u32[]{:S(2)}) %all-to-all-start.4) | async-done | bytes 1179680 | tf_op jit(solution)/shard_map/all_to_all | solution.py:42
  677.6 1.7 reduce_sum.115
  680.0 1.4 multiply_add_fusion
  681.5 1.9 fusion.12
  (47 shorter events, 5.0 us)
Async XLA Ops:
  7.2 15.5 %copy-start = (bf16[2304,576]{0,1:T(8,128)(2,1)S(1)}, bf16[2304,576]{0,1:T(8,128)(2,1)}, u32[]{:S(2)}) copy-start(bf16[2304,576]{0,1:T(8,128)(2,1)} %param.10) | copy-start | bytes 7962628
  10.7 22.9 %all-to-all-start.5 = ((s32[32,1,2]{2,1,0:T(1,128)}), s32[32,1,2]{2,1,0:T(1,128)S(1)}, u32[]{:S(2)}, u32[]{:S(2)}) async-start(s32[32,1,2]{2,1,0:T(1,128)} %bitcast.30), calls=%async_computation.5 | async-start | bytes 32768 | tf_op jit(solution)/shard_map/all_to_all | solution.py:138
  33.6 14.3 %all-to-all-start.6 = ((s32[32,1,2]{2,1,0:T(1,128)}), s32[32,1,2]{2,1,0:T(1,128)S(1)}, u32[]{:S(2)}, u32[]{:S(2)}) async-start(s32[32,1,2]{2,1,0:T(1,128)} %bitcast.33), calls=%async_computation.6 | async-start | bytes 32768 | tf_op jit(solution)/shard_map/all_to_all | solution.py:138
  47.8 8.3 %copy-start.4 = (s32[2304]{0:T(1024)S(1)}, s32[2304]{0:T(1024)}, u32[]{:S(2)}) copy-start(s32[2304]{0:T(1024)} %param.11) | copy-start | bytes 27652
  47.9 13.7 %copy-start.5 = (s32[1,2,64]{2,1,0:T(2,128)S(1)}, s32[1,2,64]{2,1,0:T(2,128)}, u32[]{:S(2)}) copy-start(s32[1,2,64]{2,1,0:T(2,128)} %param.12) | copy-start | bytes 1540
  47.9 471.8 %all-to-all-start = ((bf16[2304,8,576]{0,2,1:T(8,128)(2,1)}), bf16[2304,8,576]{0,2,1:T(8,128)(2,1)}, u32[]{:S(2)}, u32[]{:S(2)}) async-start(bf16[2304,8,576]{0,2,1:T(8,128)(2,1)} %bitcast), calls=%async_computation | async-start | bytes 42467328 | tf_op jit(solution)/shard_map/all_to_all | solution.py:111
  519.6 17.1 %all-to-all-start.7 = ((bf16[32,2,4608]{2,1,0:T(2,128)(2,1)}), bf16[32,2,4608]{2,1,0:T(2,128)(2,1)}, u32[]{:S(2)}, u32[]{:S(2)}) async-start(bf16[32,2,4608]{2,1,0:T(2,128)(2,1)} %reshape.172), calls=%async_computation.7 | async-start | bytes 1179648 | tf_op jit(solution)/shard_map/all_to_all | solution.py:137
  536.7 16.6 %all-to-all-start.8 = ((bf16[32,2,4608]{2,1,0:T(2,128)(2,1)}), bf16[32,2,4608]{2,1,0:T(2,128)(2,1)}, u32[]{:S(2)}, u32[]{:S(2)}) async-start(bf16[32,2,4608]{2,1,0:T(2,128)(2,1)} %reshape.174), calls=%async_computation.8 | async-start | bytes 1179648 | tf_op jit(solution)/shard_map/all_to_all | solution.py:137
  554.0 14.2 %all-to-all-start.2 = ((f32[32,1,128]{2,1,0:T(1,128)}), f32[32,1,128]{2,1,0:T(1,128)S(1)}, u32[]{:S(2)}, u32[]{:S(2)}) async-start(f32[32,1,128]{2,1,0:T(1,128)} %broadcast_in_dim.15), calls=%async_computation.2 | async-start | bytes 32768 | tf_op jit(solution)/shard_map/all_to_all | solution.py:16
  568.8 11.2 %all-to-all-start.1 = ((f32[32,1,128]{2,1,0:T(1,128)}), f32[32,1,128]{2,1,0:T(1,128)S(1)}, u32[]{:S(2)}, u32[]{:S(2)}) async-start(f32[32,1,128]{2,1,0:T(1,128)} %broadcast_in_dim.14), calls=%async_computation.1 | async-start | bytes 32768 | tf_op jit(solution)/shard_map/all_to_all | solution.py:16
  572.9 107.1 %reduce-scatter.2.cloned.1.call-start = ((), (), s32[]{:S(2)}) async-start(), calls=%async_computation.10 | async-start | bytes 5308416 | tf_op jit(solution)/shard_map/reduce_scatter | solution.py:145
  610.5 33.5 %all-to-all-start.3 = ((f32[32,64,144]{2,1,0:T(8,128)}), f32[32,64,144]{2,1,0:T(8,128)}, u32[]{:S(2)}, u32[]{:S(2)}) async-start(f32[32,64,144]{2,1,0:T(8,128)} %convolution_bitcast_fusion.1), calls=%async_computation.3 | async-start | bytes 4194304 | tf_op jit(solution)/shard_map/all_to_all | solution.py:42
  629.3 50.7 %copy-start.1 = (f32[256,576]{0,1:T(8,128)S(1)}, f32[256,576]{0,1:T(8,128)}, u32[]{:S(2)}) copy-start(f32[256,576]{0,1:T(8,128)} %param.16) | copy-start | bytes 1769476
  644.0 33.6 %all-to-all-start.4 = ((f32[32,64,144]{2,1,0:T(8,128)}), f32[32,64,144]{2,1,0:T(8,128)}, u32[]{:S(2)}, u32[]{:S(2)}) async-start(f32[32,64,144]{2,1,0:T(8,128)} %convolution_bitcast_fusion), calls=%async_computation.4 | async-start | bytes 4194304 | tf_op jit(solution)/shard_map/all_to_all | solution.py:42
  681.4 1.9 copy-start.2
  681.4 1.9 copy-start.3
Sparse Core Ops, SparseCore 0:
  597.9 54.0 reduce-scatter.1
